TPU v7x, 256 devices: a whole 4x4x8 slice. The times are simulated.
256 devices in a mesh: dp: 64 (over z, y, core), mp: 4 (over x).
Axes of the slice: x: 4, y: 4, z: 8, core: 2. Of those that a mesh axis runs over, the one named last changes fastest.
Arguments:
- tokens: bfloat16 [393216, 512], P('dp'), may hold values from -6 to 6
- w_uvqk: bfloat16 [512, 2048], P(None, 'mp')
- w_out: bfloat16 [512, 512], replicated, may hold values from -0.25 to 0.25
- hist_len: int32 [64, 24], P('dp'), may hold values from 64 to 256, as said below
- owner: int32 [64, 24], P('dp'), may hold values from 0 to 63, as said below
- recv_offset: int32 [64, 24], P('dp'), may hold values from 0 to 47, as said below
- block_start: int32 [64, 24], P('dp'), may hold values from 0 to 47, as said below
Outputs:
- packed_out: bfloat16 [393216, 512], P('dp', 'mp')
- user_state: bfloat16 [1536, 512], P('dp', 'mp')
Inputs may be any that keep to these rules, and one draw needn't show every extreme that they name: User (d, u) has ceil(hist_len / 128) blocks, at most 2. owner[d, u] = (p(d) + r(u mod 64)) mod 64 for two permutations p, r of the indices of dp drawn from the seed: every owner receives exactly 24 users, and one device sends at most 1 users to one owner. On some owner every received user has 2 blocks. `recv_offset`: the users of one owner occupy disjoint runs of its 48 blocks, in the order of u; on some owner they fill all 48 blocks. `block_start`: the users of one device occupy disjoint runs of its 48 blocks, in the order of u.
All inputs are finite; a program needn't handle non-finite values.
Results may differ from a plain program's by a relative error of at most 0.0059.
Values may be sent and summed in bfloat16 or wider, within the bound.
A program may use at most 128 MiB of HBM per device.

v0:
```python
import jax
import jax.numpy as jnp
from jax import lax
from jax.sharding import PartitionSpec as P

D = 512
HEADS = 4
BLOCK = 128
MAXB = 2
BLK_DEV = 48
EPS = 1e-05


def sent_to_all(shard, axis):
    count = lax.axis_size(axis)
    return lax.all_to_all(
        jnp.broadcast_to(shard[None], (count, *shard.shape)), axis, 0, 0, tiled=True
    )


def over_copies(shard, axis):
    everything = sent_to_all(shard, axis)
    return jnp.sum(everything, axis=0)


def together(arrays, axis):
    ends = [0]
    for a in arrays:
        ends.append(ends[-1] + a.size)
    subtotal = over_copies(jnp.concatenate([a.ravel() for a in arrays]), axis)
    return tuple((subtotal[b:e].reshape(a.shape) for a, b, e in zip(arrays, ends, ends[1:])))


def in_one_piece(arrays, axis, dim, along):
    widths = [a.shape[along] for a in arrays]
    both = jnp.concatenate(arrays, axis=along)
    result = lax.all_gather(both, axis, axis=dim, tiled=True)
    return tuple(jnp.split(result, [sum(widths[:k]) for k in range(1, len(widths))], axis=along))


def norm_rows(values):
    average = jnp.mean(values, axis=-1, keepdims=True)
    variance = jnp.mean(values * values, axis=-1, keepdims=True) - average * average
    return (values - average) * lax.rsqrt(variance + EPS)


def attend(query, keys, values, query_user, key_user):
    row_count, head_size = query.shape
    tile_rows = 4 * BLOCK
    back_rows = (MAXB - 1) * BLOCK
    scaling = (D // HEADS) ** (-0.5)
    keys_ext = jnp.concatenate([jnp.zeros((back_rows, head_size), keys.dtype), keys], 0)
    values_ext = jnp.concatenate([jnp.zeros((back_rows, head_size), values.dtype), values], 0)
    users_ext = jnp.concatenate([jnp.full((back_rows,), -2, jnp.int32), key_user], 0)
    query_pos = jnp.arange(tile_rows, dtype=jnp.int32)[:, None] + back_rows
    key_pos = jnp.arange(tile_rows + back_rows, dtype=jnp.int32)[None, :]

    def one_tile(start):
        query_tile = lax.dynamic_slice_in_dim(query, start, tile_rows, 0)
        key_tile = lax.dynamic_slice_in_dim(keys_ext, start, tile_rows + back_rows, 0)
        value_tile = lax.dynamic_slice_in_dim(values_ext, start, tile_rows + back_rows, 0)
        query_owner = lax.dynamic_slice_in_dim(query_user, start, tile_rows, 0)
        key_owner = lax.dynamic_slice_in_dim(users_ext, start, tile_rows + back_rows, 0)
        raw_scores = (
            lax.dot_general(
                query_tile, key_tile, (((1,), (1,)), ((), ())), preferred_element_type=jnp.float32
            )
            * scaling
        )
        allowed = (query_owner[:, None] == key_owner[None, :]) & (key_pos <= query_pos)
        weights = jnp.where(allowed, jax.nn.silu(raw_scores) / (MAXB * BLOCK), 0.0).astype(
            jnp.bfloat16
        )
        return jnp.dot(weights, value_tile, preferred_element_type=jnp.float32)

    tile_starts = jnp.arange(row_count // tile_rows, dtype=jnp.int32) * tile_rows
    return lax.map(one_tile, tile_starts).reshape(row_count, head_size)


def layer_rows(rows_in, query_user, key_user, w_uvqk, w_out):
    row_count = rows_in.shape[0]
    head_size = D // HEADS
    mp_size = lax.axis_size("mp")
    portion = lax.axis_index("mp")
    quarter = D // mp_size
    local_heads = w_uvqk.shape[1] // (4 * head_size)
    widened = rows_in.astype(jnp.float32)
    normed = norm_rows(widened).astype(jnp.bfloat16)
    projected = jax.nn.silu(jnp.dot(normed, w_uvqk, preferred_element_type=jnp.float32)).astype(
        jnp.bfloat16
    )
    pieces = projected.reshape(row_count, local_heads, 4, head_size)
    outputs = attend(pieces[:, 0, 2], pieces[:, 0, 3], pieces[:, 0, 1], query_user, key_user)
    totals = together((jnp.sum(outputs, 1), jnp.sum(outputs * outputs, 1)), "mp")
    average = totals[0] / D
    variance = totals[1] / D - average * average
    gates = pieces[:, :, 0].reshape(row_count, local_heads * head_size).astype(jnp.float32)
    gated_rows = ((outputs - average[:, None]) * lax.rsqrt(variance + EPS)[:, None] * gates).astype(
        jnp.bfloat16
    )
    every_head = lax.all_gather(gated_rows, "mp", axis=1, tiled=True)
    out_columns = lax.dynamic_slice_in_dim(w_out, portion * quarter, quarter, 1)
    mixed_rows = jnp.dot(every_head, out_columns, preferred_element_type=jnp.float32)
    residual = lax.dynamic_slice_in_dim(widened, portion * quarter, quarter, 1)
    return (mixed_rows + residual).astype(jnp.bfloat16)


def row_labels(block_user, block_fill):
    in_block = jnp.arange(BLOCK, dtype=jnp.int32)[None, :]
    row_live = (in_block < block_fill[:, None]).reshape(-1)
    row_user = jnp.broadcast_to(block_user[:, None], (block_user.shape[0], BLOCK)).reshape(-1)
    return (row_live, jnp.where(row_live, row_user, -3), jnp.where(row_live, row_user, -2))


def per_device(tokens, w_uvqk, w_out, hist_len, owner, recv_offset, block_start):
    dp_size = lax.axis_size("dp")
    mp_size = lax.axis_size("mp")
    myself = lax.axis_index("dp")
    user_count = hist_len.shape[1]
    per_pair = -(-user_count // dp_size)
    pair_cap = per_pair * MAXB
    quarter = D // mp_size
    lengths = hist_len[0]
    owners = owner[0]
    starts = block_start[0]
    counts = (lengths + BLOCK - 1) // BLOCK
    user_ids = jnp.arange(user_count, dtype=jnp.int32)
    earlier = user_ids[None, :] < user_ids[:, None]
    same_owner = (owners[:, None] == owners[None, :]) & earlier
    in_pair = jnp.sum(jnp.where(same_owner, counts[None, :], 0), axis=1)
    slot_ids = jnp.arange(pair_cap, dtype=jnp.int32)
    device_ids = jnp.arange(dp_size, dtype=jnp.int32)
    slot_step = slot_ids[None, :, None] - in_pair[None, None, :]
    sending = (
        (owners[None, None, :] == device_ids[:, None, None])
        & (slot_step >= 0)
        & (slot_step < counts[None, None, :])
    )
    send_block = jnp.sum(jnp.where(sending, starts[None, None, :] + slot_step, 0), axis=2)
    all_len, all_owner, all_offset = in_one_piece((hist_len, owner, recv_offset), "dp", 0, 1)
    all_counts = (all_len + BLOCK - 1) // BLOCK
    all_before = (all_owner[:, :, None] == all_owner[:, None, :]) & earlier[None]
    all_in_pair = jnp.sum(jnp.where(all_before, all_counts[:, None, :], 0), axis=2)
    owned = all_owner == myself
    flat_owned = owned.reshape(-1)
    flat_len = all_len.reshape(-1)
    flat_offset = all_offset.reshape(-1)
    flat_counts = all_counts.reshape(-1)
    flat_in_pair = all_in_pair.reshape(-1)
    candidate_ids = jnp.arange(dp_size * user_count, dtype=jnp.int32)
    source_ids = candidate_ids // user_count
    block_ids = jnp.arange(BLK_DEV, dtype=jnp.int32)
    land_step = block_ids[:, None] - flat_offset[None, :]
    landed = flat_owned[None, :] & (land_step >= 0) & (land_step < flat_counts[None, :])
    slot_index = jnp.sum(
        jnp.where(landed, source_ids[None, :] * pair_cap + flat_in_pair[None, :] + land_step, 0),
        axis=1,
    )
    owned_user = jnp.sum(jnp.where(landed, candidate_ids[None, :], 0), axis=1)
    owned_fill = jnp.sum(
        jnp.where(landed, jnp.clip(flat_len[None, :] - land_step * BLOCK, 0, BLOCK), 0), axis=1
    )
    owned_live, owned_query, owned_key = row_labels(owned_user, owned_fill)
    local_step = block_ids[:, None] - starts[None, :]
    within = (local_step >= 0) & (local_step < counts[None, :])
    local_user = jnp.sum(jnp.where(within, user_ids[None, :], 0), axis=1)
    local_fill = jnp.sum(
        jnp.where(within, jnp.clip(lengths[None, :] - local_step * BLOCK, 0, BLOCK), 0), axis=1
    )
    local_live, local_query, local_key = row_labels(local_user, local_fill)
    results = layer_rows(tokens, local_query, local_key, w_uvqk, w_out)
    state = jnp.take(results, starts * BLOCK + lengths - 1, axis=0)
    outgoing = jnp.take(results.reshape(BLK_DEV, BLOCK, quarter), send_block, axis=0)
    arrived = lax.all_to_all(outgoing, "dp", split_axis=0, concat_axis=0, tiled=True)
    gathered = jnp.take(
        arrived.reshape(dp_size * pair_cap, BLOCK, quarter), slot_index, axis=0
    ).reshape(BLK_DEV * BLOCK, quarter)
    packed = jnp.where(owned_live[:, None], gathered, jnp.zeros_like(gathered))
    return (packed, state)


def solution(mesh):
    in_specs = (
        P("dp", None),
        P(None, "mp"),
        P(),
        P("dp", None),
        P("dp", None),
        P("dp", None),
        P("dp", None),
    )
    out_specs = (P("dp", "mp"), P("dp", "mp"))
    return jax.shard_map(
        per_device, mesh=mesh, in_specs=in_specs, out_specs=out_specs, check_vma=False
    )
```

profile of v0, /device:TPU:1, one launch (start us, length us, event | category | flops | bytes accessed | tf_op | source)
XLA Modules:
  0.0 370.8 jit_solution(17628559279992237693)
XLA Ops:
  7.2 4.8 %convert_reduce_fusion = (f32[6144]{0:T(1024)S(1)}, f32[6144]{0:T(1024)S(1)}) fusion(bf16[6144,512]{1,0:T(8,128)(2,1)} %param.9), kind=kLoop, calls=%fused_computation.31 | loop fusion | flops 12570624 | bytes 6340608 | tf_op jit(solution)/shard_map/reduce_sum | solution.py:42
  12.0 8.0 %multiply_convert_fusion = bf16[6144,512]{0,1:T(8,128)(2,1)S(1)} fusion(bf16[512,512]{1,0:T(8,128)(2,1)S(1)} %copy-done, bf16[6144,512]{1,0:T(8,128)(2,1)S(1)} %copy-done.2, f32[6144]{0:T(1024)S(1)} %get-tuple-element.108, f32[6144]{0:T(1024)S(1)} %get-tuple-element.107), kind=kOutput, calls=%fused_computation.28 | convolution fusion | flops 3249537024 | bytes 13156352 | tf_op jit(solution)/shard_map/dot_general | solution.py:89
  20.0 2.3 fusion.59
  22.3 1.3 copy-done.3
  23.7 2.6 copy.50
  26.3 2.6 copy.51
  28.9 2.8 concatenate.17
  31.7 1.3 concatenate.18
  33.0 1.6 copy.49
  34.6 0.1 select_reduce_fusion.5
  34.7 78.6 %while.11 = (s32[]{:T(128)}, f32[12,512,128]{2,1,0:T(8,128)}, s32[12]{0:T(128)S(1)}, s32[6144]{0:T(1024)S(1)}, s32[6272]{0:T(1024)S(1)}, /*index=5*/bf16[6144,12...) while((s32[]{:T(128)}, f32[12,512,128]{2,1,0:T(8,128)}, ...), condition=%wide.region_10.11_spmd.clone, body=%wide.region_9.10_spmd.clone.sunk | while | flops 171377152 | bytes 741060 | solution.py:77
  34.8 0.6 dynamic_slice.53
  38.7 2.6 fusion.70
  41.3 0.6 dynamic_slice.53
  45.3 2.6 fusion.70
  47.9 0.6 dynamic_slice.53
  51.8 2.6 fusion.70
  54.4 0.6 dynamic_slice.53
  58.4 2.6 fusion.70
  61.0 0.6 dynamic_slice.53
  64.9 2.6 fusion.70
  67.5 0.6 dynamic_slice.53
  71.5 2.6 fusion.70
  74.1 0.6 dynamic_slice.53
  78.0 2.6 fusion.70
  80.6 0.6 dynamic_slice.53
  84.5 2.6 fusion.70
  87.2 0.6 dynamic_slice.53
  91.1 2.6 fusion.70
  93.7 0.6 dynamic_slice.53
  97.7 2.6 fusion.70
  100.3 0.6 dynamic_slice.53
  104.2 2.6 fusion.70
  106.8 0.6 dynamic_slice.53
  110.8 2.6 fusion.70
  113.4 3.6 fusion.58
  117.0 0.8 broadcast_in_dim.174
  117.8 4.8 %all-to-all-start = ((f32[4,1,12288]{2,1,0:T(1,128)}), f32[4,1,12288]{2,1,0:T(1,128)S(1)}, u32[]{:S(2)}, u32[]{:S(2)}) async-start(f32[4,1,12288]{2,1,0:T(1,128)} %broadcast_in_dim.174), calls=%async_computation | async-start | bytes 393216 | tf_op jit(solution)/shard_map/all_to_all | solution.py:16
  122.6 3.5 copy.46
  126.2 1.6 all-to-all-done
  127.8 0.2 reduce_sum.129
  128.0 4.0 %fusion.30 = bf16[6144,128]{0,1:T(8,128)(2,1)} fusion(f32[6144,128]{0,1:T(8,128)} %copy.46, bf16[6144,1,4,128]{0,3,2,1:T(8,128)(2,1)} %bitcast.68, f32[6144]{0:T(1024)S(1)} %get-tuple-element.102, f32[6144]{0:T(1024)S(1)} %get-tuple-element.101), kind=kLoop, calls=%fused_computation.39 | loop fusion | flops 3932160 | bytes 6340608 | tf_op jit(solution)/shard_map/convert_element_type | solution.py:98
  132.0 9.2 %convert_element_type.24 = f32[6144,512]{1,0:T(8,128)} convert(bf16[6144,512]{1,0:T(8,128)(2,1)} %param.9) | non-fusion elementwise | flops 3145728 | bytes 18874368 | tf_op jit(solution)/shard_map/convert_element_type | solution.py:87
  141.2 0.2 select_reduce_fusion.6
  141.5 0.1 select_reduce_fusion.3
  141.6 0.1 copy.47
  141.7 0.1 reshape.360
  141.9 0.1 copy.41
  142.0 60.7 %all-gather.3.cloned.1.call-done = bf16[6144,512]{0,1:T(8,128)(2,1)} async-done(((bf16[6144,128]{0,1:T(8,128)(2,1)}), bf16[6144,512]{0,1:T(8,128)(2,1)}) %all-gather.3.cloned.1.call-update) | async-done | bytes 6291472 | tf_op jit(solution)/shard_map/all_gather | solution.py:101
  202.7 5.6 %fusion.26 = bf16[6144,128]{1,0:T(8,128)(2,1)S(1)} fusion(bf16[6144,512]{0,1:T(8,128)(2,1)} %all-gather.3.cloned.1.call-done, f32[6144,512]{1,0:T(8,128)} %convert_element_type.24, s32[]{:T(128)S(6)} %select_n.164, bf16[512,512]{1,0:T(8,128)(2,1)} %param.11), kind=kOutput, calls=%fused_computation.33 | convolution fusion | flops 806879232 | bytes 11142144 | tf_op jit(solution)/shard_map/dot_general | solution.py:103
  208.4 3.1 gather_fusion
  211.4 4.6 %broadcast_select_fusion = bf16[64,2,128,128]{3,2,1,0:T(8,128)(2,1)} fusion(bf16[64,2,128,128]{3,2,1,0:T(8,128)(2,1)} %bitcast.65, pred[64,2]{1,0:T(8,128)(4,1)S(1)} %copy.41), kind=kLoop, calls=%fused_computation.37 | loop fusion | flops 2097152 | bytes 8388736 | tf_op jit(solution)/shard_map/jit(_take)/select_n | solution.py:173
  216.0 11.2 %all-to-all-start.1 = ((bf16[64,2,128,128]{3,2,1,0:T(8,128)(2,1)}), bf16[64,2,128,128]{3,2,1,0:T(8,128)(2,1)}, u32[]{:S(2)}, u32[]{:S(2)}) async-start(bf16[64,2,128,128]{3,2,1,0:T(8,128)(2,1)} %broadcast_select_fusion), calls=%async_computation.1 | async-start | bytes 8388608 | tf_op jit(solution)/shard_map/all_to_all | solution.py:174
  227.3 125.6 %all-gather = s32[64,1,72]{2,1,0:T(1,128)S(1)} all-gather(s32[1,1,72]{2,1,0:T(1,128)S(1)} %add_bitcast_fusion), channel_id=1, replica_groups=mesh['dp'=64,'mp'=4] {'dp'}, dimensions={0}, use_global_device_ids=true | all-gather | bytes 18720 | tf_op jit(solution)/shard_map/all_gather | solution.py:37
  352.9 0.1 fusion.60
  353.0 0.1 lt.161
  353.2 0.2 select_reduce_fusion.1
  353.4 0.1 broadcast_in_dim_reshape.2
  353.8 0.1 and.104
  353.9 0.3 select_reduce_fusion.2
  354.4 0.6 gather_fusion.2
  355.0 0.7 broadcast_select_fusion.1
  355.6 3.1 gather_fusion.1
  358.7 5.2 %fusion.31 = bf16[6144,128]{1,0:T(8,128)(2,1)} fusion(bf16[48,128,128]{2,1,0:T(8,128)(2,1)S(1)} %gather_fusion.1, pred[6144]{0:T(1024)(128)(4,1)S(1)} %get-tuple-element.114, pred[6144]{0:T(1024)(128)(4,1)S(1)} %get-tuple-element.113), kind=kLoop, calls=%fused_computation.43 | loop fusion | flops 1572864 | bytes 3158016 | tf_op jit(solution)/shard_map/jit(_where)/select_n | solution.py:178
  (89 shorter events, 3.0 us)
Async XLA Ops:
  7.2 4.8 %copy-start = (bf16[512,512]{1,0:T(8,128)(2,1)S(1)}, bf16[512,512]{1,0:T(8,128)(2,1)}, u32[]{:S(2)}) copy-start(bf16[512,512]{1,0:T(8,128)(2,1)} %param.10) | copy-start | bytes 1572868
  7.2 4.8 %copy-start.2 = (bf16[6144,512]{1,0:T(8,128)(2,1)S(1)}, bf16[6144,512]{1,0:T(8,128)(2,1)}, u32[]{:S(2)}) copy-start(bf16[6144,512]{1,0:T(8,128)(2,1)} %param.9) | copy-start | bytes 18874372
  20.0 3.7 copy-start.3
  28.9 2.8 copy-start.4
  31.7 2.8 copy-start.6
  31.7 2.8 copy-start.7
  117.8 10.0 %all-to-all-start = ((f32[4,1,12288]{2,1,0:T(1,128)}), f32[4,1,12288]{2,1,0:T(1,128)S(1)}, u32[]{:S(2)}, u32[]{:S(2)}) async-start(f32[4,1,12288]{2,1,0:T(1,128)} %broadcast_in_dim.174), calls=%async_computation | async-start | bytes 393216 | tf_op jit(solution)/shard_map/all_to_all | solution.py:16
  122.6 80.1 %all-gather.3.cloned.1.call-start = ((), (), s32[]{:S(2)}) async-start(), calls=%async_computation.2 | async-start | bytes 7864320 | tf_op jit(solution)/shard_map/all_gather | solution.py:101
  132.0 9.2 %copy-start.5 = (s32[1,24]{1,0:T(1,128)S(1)}, s32[1,24]{1,0:T(1,128)}, u32[]{:S(2)}) copy-start(s32[1,24]{1,0:T(1,128)} %param.13) | copy-start | bytes 292
  216.0 11.2 %copy-start.8 = (s32[1,24]{1,0:T(1,128)S(1)}, s32[1,24]{1,0:T(1,128)}, u32[]{:S(2)}) copy-start(s32[1,24]{1,0:T(1,128)} %param.14) | copy-start | bytes 292
  216.0 139.6 %all-to-all-start.1 = ((bf16[64,2,128,128]{3,2,1,0:T(8,128)(2,1)}), bf16[64,2,128,128]{3,2,1,0:T(8,128)(2,1)}, u32[]{:S(2)}, u32[]{:S(2)}) async-start(bf16[64,2,128,128]{3,2,1,0:T(8,128)(2,1)} %broadcast_select_fusion), calls=%async_computation.1 | async-start | bytes 8388608 | tf_op jit(solution)/shard_map/all_to_all | solution.py:174
  355.6 8.3 %copy-start.1 = (bf16[512,512]{1,0:T(8,128)(2,1)S(1)}, bf16[512,512]{1,0:T(8,128)(2,1)}, u32[]{:S(2)}) copy-start(bf16[512,512]{1,0:T(8,128)(2,1)} %param.10) | copy-start | bytes 1572868
Sparse Core Ops, SparseCore 0:
  132.1 70.5 all-gather.2
where the time goes:
time: 372 us; the launch traced here: 371 us
  blocking collectives  126 us (34%)
  waiting for transfers between devices  62.4 us (17%)
  matrix products  45 us (12%)
  loops' own time  37.9 us (10%)
  local copies, waits for them, and re-layouts  35.9 us (10%)
  other arithmetic  33.7 us (9%)
  starting transfers between devices  16 us (4%)
  between operations  14.3 us (4%)
    all_gather x1, blocking collectives, in_one_piece(): result = lax.all_gather(both, axis, axis=dim, tiled=True)  126 us
    all_gather x1, waiting for transfers between devices, layer_rows(): every_head = lax.all_gather(gated_rows, 'mp', axis=1, tiled=True)  60.7 us
    another operation x1, loops' own time, attend(): return lax.map(one_tile, tile_starts).reshape(row_count, head_size)  37.9 us
    dot_general x12, matrix products, one_tile(): return jnp.dot(weights, value_tile, preferred_element_type=jnp.float32)  31.4 us
    all_to_all x1, starting transfers between devices, per_device(): lax.all_to_all(outgoing, 'dp', split_axis=0, concat_axis=0, tiled=True)  11.2 us
    convert_element_type x1, other arithmetic, layer_rows(): widened = rows_in.astype(jnp.float32)  9.17 us
    unnamed x21, local copies, waits for them, and re-layouts  8.13 us
    dot_general x1, matrix products, layer_rows(): jnp.dot(normed, w_uvqk, preferred_element_type=jnp.float32)  7.98 us
  transfers between devices with their start and end apart: 3, of which 2 were waited for; matrix products, arithmetic and copies ran while one was open for 4% of the time, Pallas kernels for 0%

commit v1 on v0

--- a/solution.py
+++ b/solution.py
@@ -98,7 +98,8 @@
     gated_rows = ((outputs - average[:, None]) * lax.rsqrt(variance + EPS)[:, None] * gates).astype(
         jnp.bfloat16
     )
-    every_head = lax.all_gather(gated_rows, "mp", axis=1, tiled=True)
+    stack = jnp.stack([gated_rows] * lax.axis_size("mp"))
+    every_head = jnp.concatenate(lax.all_to_all(stack, "mp", 0, 0), axis=1)
     out_columns = lax.dynamic_slice_in_dim(w_out, portion * quarter, quarter, 1)
     mixed_rows = jnp.dot(every_head, out_columns, preferred_element_type=jnp.float32)
     residual = lax.dynamic_slice_in_dim(widened, portion * quarter, quarter, 1)

time: 372 us -> 369 us (level)
  between operations: 14.3 us -> 0.96 us
  starting transfers between devices: 16 us -> 26 us
    all_gather x1 -> x0, waiting for transfers between devices: 60.7 us -> none  [layer_rows(): every_head = lax.all_gather(gated_rows, 'mp', axis=1, tiled=True)]
    all_to_all x0 -> x1, waiting for transfers between devices: none -> 58.4 us  [layer_rows(): every_head = jnp.concatenate(lax.all_to_all(stack, 'mp', 0, 0), axis=1)]
    all_to_all x0 -> x1, starting transfers between devices: none -> 5.46 us  [layer_rows(): every_head = jnp.concatenate(lax.all_to_all(stack, 'mp', 0, 0), axis=1)]
    all_to_all x1, starting transfers between devices: 11.2 us -> 15.7 us  [per_device(): lax.all_to_all(outgoing, 'dp', split_axis=0, concat_axis=0, tiled=True)]
where the time goes in v1:
time: 369 us; the launch traced here: 367 us
  blocking collectives  126 us (34%)
  waiting for transfers between devices  60.1 us (16%)
  matrix products  45 us (12%)
  local copies, waits for them, and re-layouts  39.3 us (11%)
  loops' own time  37.9 us (10%)
  other arithmetic  32.5 us (9%)
  starting transfers between devices  26 us (7%)
    all_gather x1, blocking collectives, in_one_piece(): result = lax.all_gather(both, axis, axis=dim, tiled=True)  126 us
    all_to_all x1, waiting for transfers between devices, layer_rows(): every_head = jnp.concatenate(lax.all_to_all(stack, 'mp', 0, 0), axis=1)  58.4 us
    another operation x1, loops' own time, attend(): return lax.map(one_tile, tile_starts).reshape(row_count, head_size)  37.9 us
    dot_general x12, matrix products, one_tile(): return jnp.dot(weights, value_tile, preferred_element_type=jnp.float32)  31.4 us
    all_to_all x1, starting transfers between devices, per_device(): lax.all_to_all(outgoing, 'dp', split_axis=0, concat_axis=0, tiled=True)  15.7 us
    convert_element_type x1, other arithmetic, layer_rows(): widened = rows_in.astype(jnp.float32)  9.17 us
    unnamed x21, local copies, waits for them, and re-layouts  8.14 us
    dot_general x1, matrix products, layer_rows(): jnp.dot(normed, w_uvqk, preferred_element_type=jnp.float32)  7.98 us
  transfers between devices with their start and end apart: 3, of which 2 were waited for; matrix products, arithmetic and copies ran while one was open for 4% of the time, Pallas kernels for 0%

profile of v1, /device:TPU:1, one launch (start us, length us, event | category | flops | bytes accessed | tf_op | source)
XLA Modules:
  0.0 367.4 jit_solution(1588174501374040545)
XLA Ops:
  0.7 4.8 %convert_reduce_fusion = (f32[6144]{0:T(1024)S(1)}, f32[6144]{0:T(1024)S(1)}) fusion(bf16[6144,512]{1,0:T(8,128)(2,1)} %param.9), kind=kLoop, calls=%fused_computation.31 | loop fusion | flops 12570624 | bytes 6340608 | tf_op jit(solution)/shard_map/reduce_sum | solution.py:42
  5.5 8.0 %multiply_convert_fusion = bf16[6144,512]{0,1:T(8,128)(2,1)S(1)} fusion(bf16[512,512]{1,0:T(8,128)(2,1)S(1)} %copy-done, bf16[6144,512]{1,0:T(8,128)(2,1)S(1)} %copy-done.2, f32[6144]{0:T(1024)S(1)} %get-tuple-element.108, f32[6144]{0:T(1024)S(1)} %get-tuple-element.107), kind=kOutput, calls=%fused_computation.28 | convolution fusion | flops 3249537024 | bytes 13156352 | tf_op jit(solution)/shard_map/dot_general | solution.py:89
  13.5 2.3 fusion.59
  15.8 1.3 copy-done.3
  17.1 2.6 copy.51
  19.7 2.6 copy.52
  22.3 2.8 concatenate.17
  25.1 1.3 concatenate.18
  26.4 1.6 copy.50
  28.0 0.1 select_reduce_fusion.5
  28.2 78.6 %while.11 = (s32[]{:T(128)}, f32[12,512,128]{2,1,0:T(8,128)}, s32[12]{0:T(128)S(1)}, s32[6144]{0:T(1024)S(1)}, s32[6272]{0:T(1024)S(1)}, /*index=5*/bf16[6144,12...) while((s32[]{:T(128)}, f32[12,512,128]{2,1,0:T(8,128)}, ...), condition=%wide.region_10.11_spmd.clone, body=%wide.region_9.10_spmd.clone.sunk | while | flops 171377152 | bytes 741060 | solution.py:77
  28.2 0.6 dynamic_slice.53
  32.1 2.6 fusion.70
  34.7 0.6 dynamic_slice.53
  38.7 2.6 fusion.70
  41.3 0.6 dynamic_slice.53
  45.2 2.6 fusion.70
  47.8 0.6 dynamic_slice.53
  51.8 2.6 fusion.70
  54.4 0.6 dynamic_slice.53
  58.3 2.6 fusion.70
  60.9 0.6 dynamic_slice.53
  64.9 2.6 fusion.70
  67.5 0.6 dynamic_slice.53
  71.4 2.6 fusion.70
  74.0 0.6 dynamic_slice.53
  78.0 2.6 fusion.70
  80.6 0.6 dynamic_slice.53
  84.5 2.6 fusion.70
  87.1 0.6 dynamic_slice.53
  91.1 2.6 fusion.70
  93.7 0.6 dynamic_slice.53
  97.6 2.6 fusion.70
  100.2 0.6 dynamic_slice.53
  104.2 2.6 fusion.70
  106.8 3.6 fusion.58
  110.4 0.8 broadcast_in_dim.174
  111.2 4.8 %all-to-all-start = ((f32[4,1,12288]{2,1,0:T(1,128)}), f32[4,1,12288]{2,1,0:T(1,128)S(1)}, u32[]{:S(2)}, u32[]{:S(2)}) async-start(f32[4,1,12288]{2,1,0:T(1,128)} %broadcast_in_dim.174), calls=%async_computation | async-start | bytes 393216 | tf_op jit(solution)/shard_map/all_to_all | solution.py:16
  116.0 3.5 copy.47
  119.6 1.6 all-to-all-done
  121.2 0.2 reduce_sum.129
  121.4 2.8 fusion.30
  124.3 3.5 stack.2
  127.8 5.5 %all-to-all-start.1 = ((bf16[4,6144,128]{1,2,0:T(8,128)(2,1)}), bf16[4,6144,128]{1,2,0:T(8,128)(2,1)}, u32[]{:S(2)}, u32[]{:S(2)}) async-start(bf16[4,6144,128]{1,2,0:T(8,128)(2,1)} %stack.2), calls=%async_computation.1 | async-start | bytes 12582912 | tf_op jit(solution)/shard_map/all_to_all | solution.py:102
  133.2 9.2 %convert_element_type.28 = f32[6144,512]{1,0:T(8,128)} convert(bf16[6144,512]{1,0:T(8,128)(2,1)} %param.9) | non-fusion elementwise | flops 3145728 | bytes 18874368 | tf_op jit(solution)/shard_map/convert_element_type | solution.py:87
  142.4 0.2 select_reduce_fusion.6
  142.7 0.1 select_reduce_fusion.3
  142.8 0.1 copy.48
  142.9 0.1 reshape.385
  143.1 0.1 copy.42
  143.2 58.4 %all-to-all-done.1 = bf16[4,6144,128]{1,2,0:T(8,128)(2,1)} async-done(((bf16[4,6144,128]{1,2,0:T(8,128)(2,1)}), bf16[4,6144,128]{1,2,0:T(8,128)(2,1)}, u32[]{:S(2)}, u32[]{:S(2)}) %all-to-all-start.1) | async-done | bytes 6291488 | tf_op jit(solution)/shard_map/all_to_all | solution.py:102
  201.6 5.6 %fusion.26 = bf16[6144,128]{1,0:T(8,128)(2,1)S(1)} fusion(bf16[6144,512]{0,1:T(8,128)(2,1)} %bitcast.17, f32[6144,512]{1,0:T(8,128)} %convert_element_type.28, s32[]{:T(128)S(6)} %select_n.164, bf16[512,512]{1,0:T(8,128)(2,1)} %param.11), kind=kOutput, calls=%fused_computation.33 | convolution fusion | flops 806879232 | bytes 11142144 | tf_op jit(solution)/shard_map/dot_general | solution.py:104
  207.3 3.1 gather_fusion
  210.3 4.6 %broadcast_select_fusion = bf16[64,2,128,128]{3,2,1,0:T(8,128)(2,1)} fusion(bf16[64,2,128,128]{3,2,1,0:T(8,128)(2,1)} %bitcast.68, pred[64,2]{1,0:T(8,128)(4,1)S(1)} %copy.42), kind=kLoop, calls=%fused_computation.37 | loop fusion | flops 2097152 | bytes 8388736 | tf_op jit(solution)/shard_map/jit(_take)/select_n | solution.py:174
  214.9 15.7 %all-to-all-start.2 = ((bf16[64,2,128,128]{3,2,1,0:T(8,128)(2,1)}), bf16[64,2,128,128]{3,2,1,0:T(8,128)(2,1)}, u32[]{:S(2)}, u32[]{:S(2)}) async-start(bf16[64,2,128,128]{3,2,1,0:T(8,128)(2,1)} %broadcast_select_fusion), calls=%async_computation.2 | async-start | bytes 8388608 | tf_op jit(solution)/shard_map/all_to_all | solution.py:175
  230.7 125.6 %all-gather = s32[64,1,72]{2,1,0:T(1,128)S(1)} all-gather(s32[1,1,72]{2,1,0:T(1,128)S(1)} %add_bitcast_fusion), channel_id=1, replica_groups=mesh['dp'=64,'mp'=4] {'dp'}, dimensions={0}, use_global_device_ids=true | all-gather | bytes 18720 | tf_op jit(solution)/shard_map/all_gather | solution.py:37
  356.4 0.1 lt.161
  356.6 0.2 select_reduce_fusion.1
  357.2 0.1 and.104
  357.3 0.3 select_reduce_fusion.2
  357.8 0.6 gather_fusion.2
  358.4 0.7 broadcast_select_fusion.1
  359.1 3.1 gather_fusion.1
  362.2 5.2 %fusion.31 = bf16[6144,128]{1,0:T(8,128)(2,1)} fusion(bf16[48,128,128]{2,1,0:T(8,128)(2,1)S(1)} %gather_fusion.1, pred[6144]{0:T(1024)(128)(4,1)S(1)} %get-tuple-element.114, pred[6144]{0:T(1024)(128)(4,1)S(1)} %get-tuple-element.113), kind=kLoop, calls=%fused_computation.43 | loop fusion | flops 1572864 | bytes 3158016 | tf_op jit(solution)/shard_map/jit(_where)/select_n | solution.py:179
  (89 shorter events, 3.1 us)
Async XLA Ops:
  0.6 4.8 %copy-start = (bf16[512,512]{1,0:T(8,128)(2,1)S(1)}, bf16[512,512]{1,0:T(8,128)(2,1)}, u32[]{:S(2)}) copy-start(bf16[512,512]{1,0:T(8,128)(2,1)} %param.10) | copy-start | bytes 1572868
  0.7 4.8 %copy-start.2 = (bf16[6144,512]{1,0:T(8,128)(2,1)S(1)}, bf16[6144,512]{1,0:T(8,128)(2,1)}, u32[]{:S(2)}) copy-start(bf16[6144,512]{1,0:T(8,128)(2,1)} %param.9) | copy-start | bytes 18874372
  13.5 3.6 copy-start.3
  22.3 2.8 copy-start.4
  25.1 2.8 copy-start.6
  25.1 2.8 copy-start.7
  111.2 10.0 %all-to-all-start = ((f32[4,1,12288]{2,1,0:T(1,128)}), f32[4,1,12288]{2,1,0:T(1,128)S(1)}, u32[]{:S(2)}, u32[]{:S(2)}) async-start(f32[4,1,12288]{2,1,0:T(1,128)} %broadcast_in_dim.174), calls=%async_computation | async-start | bytes 393216 | tf_op jit(solution)/shard_map/all_to_all | solution.py:16
  127.8 73.9 %all-to-all-start.1 = ((bf16[4,6144,128]{1,2,0:T(8,128)(2,1)}), bf16[4,6144,128]{1,2,0:T(8,128)(2,1)}, u32[]{:S(2)}, u32[]{:S(2)}) async-start(bf16[4,6144,128]{1,2,0:T(8,128)(2,1)} %stack.2), calls=%async_computation.1 | async-start | bytes 12582912 | tf_op jit(solution)/shard_map/all_to_all | solution.py:102
  133.2 9.2 %copy-start.5 = (s32[1,24]{1,0:T(1,128)S(1)}, s32[1,24]{1,0:T(1,128)}, u32[]{:S(2)}) copy-start(s32[1,24]{1,0:T(1,128)} %param.13) | copy-start | bytes 292
  214.9 15.7 %copy-start.8 = (s32[1,24]{1,0:T(1,128)S(1)}, s32[1,24]{1,0:T(1,128)}, u32[]{:S(2)}) copy-start(s32[1,24]{1,0:T(1,128)} %param.14) | copy-start | bytes 292
  214.9 144.2 %all-to-all-start.2 = ((bf16[64,2,128,128]{3,2,1,0:T(8,128)(2,1)}), bf16[64,2,128,128]{3,2,1,0:T(8,128)(2,1)}, u32[]{:S(2)}, u32[]{:S(2)}) async-start(bf16[64,2,128,128]{3,2,1,0:T(8,128)(2,1)} %broadcast_select_fusion), calls=%async_computation.2 | async-start | bytes 8388608 | tf_op jit(solution)/shard_map/all_to_all | solution.py:175
  359.0 8.3 %copy-start.1 = (bf16[512,512]{1,0:T(8,128)(2,1)S(1)}, bf16[512,512]{1,0:T(8,128)(2,1)}, u32[]{:S(2)}) copy-start(bf16[512,512]{1,0:T(8,128)(2,1)} %param.10) | copy-start | bytes 1572868
